TPU v7x, 32 devices: a whole 2x2x4 slice. The times are simulated.
32 devices in a mesh: section: 16 (over z, y, x), tensor: 2 (over core).
Axes of the slice: x: 2, y: 2, z: 4, core: 2. Of those that a mesh axis runs over, the one named last changes fastest.
Arguments:
- hidden_in: bfloat16 [128, 8192], P(None, 'tensor'), may hold values from -36 to 36
- segment_ids: int32 [4, 32], replicated, may hold values from 0 to 7, never falling along the last dimension, each value on 1 to 8 neighbouring positions
- segment_job: int32 [4, 8], replicated, may hold values from 0 to 5
- job_adapter: int32 [6], replicated, may hold values from 0 to 3
- owner: int32 [16], P('section'), may hold values from 0 to 1
- frozen: bfloat16 [16, 8192, 4096], P('section', None, 'tensor'), may hold values from -0.0625 to 0.0625
- norm_gain: bfloat16 [16, 4096], P('section'), may hold values from 0.3984375 to 1.59375
- inbox_down: bfloat16 [16, 2, 4096, 128], P('section', 'tensor'), may hold values from -0.0625 to 0.0625
- inbox_up: bfloat16 [16, 2, 128, 4096], P('section', 'tensor'), may hold values from -1 to 1
Outputs:
- section_out: bfloat16 [16, 128, 4096], P('section', None, 'tensor')
Inputs may be any that keep to these rules, and one draw needn't show every extreme that they name: `segment_ids`: within each micro-batch the segment numbers never fall, and each of the 8 segments has 1 to 8 tokens.
All inputs are finite; a program needn't handle non-finite values.
Results may differ from a plain program's by a relative error of at most 0.02.
Values may be sent and summed in bfloat16 or wider, within the bound.
A program may use at most 128 MiB of HBM per device.

v0:
```python
import jax
import jax.numpy as jnp
from jax import lax
from jax.sharding import PartitionSpec as P

R = 32


epsilon = 1e-05


def spread(block, axis, owner):
    block = jnp.where(lax.axis_index(axis) == owner, block, jnp.zeros_like(block))
    return lax.psum(block, axis)


def from_partner(value, axis, bit):
    mask = 2**bit
    pairs = [(source, source ^ mask) for source in range(lax.axis_size(axis))]
    return lax.ppermute(value, axis, pairs)


def shifted(value, axis, steps):
    count = lax.axis_size(axis)
    first, last = (max(0, -steps), min(count, count - steps))
    return lax.ppermute(value, axis, [(source, source + steps) for source in range(first, last)])


def product(left, right):
    return jnp.dot(left, right, preferred_element_type=jnp.float32)


def both_halves(own_part, other_part, pair_side):
    lower_part = jnp.where(pair_side == 0, own_part, other_part)
    upper_part = jnp.where(pair_side == 0, other_part, own_part)
    return (lower_part, upper_part)


def local(
    hidden_in, segment_ids, segment_job, job_adapter, owner, frozen, norm_gain, inbox_down, inbox_up
):
    tensors = lax.axis_size("tensor")
    sections = lax.axis_size("section")
    levels = sections // 2
    piece_cols = frozen.shape[2]
    half_width = norm_gain.shape[1]
    full_width = 2 * half_width
    rank_cols = inbox_down.shape[3]
    unit_count = segment_ids.shape[0]
    unit_rows = segment_ids.shape[1]
    position = lax.axis_index("section")
    pair_side = position % 2
    section_level = position // 2
    shard_index = lax.axis_index("tensor")
    down_half, up_half = (
        spread(inbox_down[0, 0], "tensor", owner[0]),
        spread(inbox_up[0, 0], "tensor", owner[0]),
    )
    up_own = lax.dynamic_slice_in_dim(up_half, shard_index * piece_cols, piece_cols, 1)
    split_weight = frozen[0].reshape(tensors, 2, piece_cols, piece_cols)
    weight_low = split_weight[:, 0].reshape(half_width, piece_cols)
    weight_high = split_weight[:, 1].reshape(half_width, piece_cols)
    gain_own = norm_gain[0]
    down_other, gain_other = from_partner((down_half, gain_own), "section", 0)
    down_low, down_high = both_halves(down_half, down_other, pair_side)
    gain_low, gain_high = both_halves(gain_own, gain_other, pair_side)
    gain_low = gain_low.astype(jnp.float32)[None, :]
    gain_high = gain_high.astype(jnp.float32)[None, :]
    seg_hit = segment_ids[:, :, None] == lax.broadcasted_iota(
        jnp.int32, (1, 1, segment_job.shape[1]), 2
    )
    token_job = jnp.sum(jnp.where(seg_hit, segment_job[:, None, :], 0), axis=2)
    job_hit = token_job[:, :, None] == lax.broadcasted_iota(
        jnp.int32, (1, 1, job_adapter.shape[0]), 2
    )
    token_adapter = jnp.sum(jnp.where(job_hit, job_adapter[None, None, :], 0), axis=2)
    slot_of_column = lax.broadcasted_iota(jnp.int32, (1, rank_cols), 1) // R
    zero_piece = jnp.zeros((unit_rows, piece_cols), jnp.bfloat16)
    zero_rank = jnp.zeros((unit_rows, rank_cols), jnp.float32)
    results = jnp.zeros((unit_count * unit_rows, piece_cols), jnp.bfloat16)

    def pipe_step(step_turn, carry):
        incoming, incoming_other, results = carry
        unit_index = step_turn - section_level
        active = jnp.logical_and(unit_index >= 0, unit_index < unit_count)
        unit_slot = jnp.clip(unit_index, 0, unit_count - 1)
        source = lax.dynamic_slice_in_dim(
            hidden_in, jnp.clip(step_turn, 0, unit_count - 1) * unit_rows, unit_rows, 0
        )
        own_source = lax.dynamic_slice_in_dim(source, pair_side * piece_cols, piece_cols, 1)
        own_piece = jnp.where(section_level == 0, own_source, incoming)
        other_piece = from_partner(own_piece, "section", 0)
        own_half, other_half = (
            lax.all_gather(own_piece, "tensor", axis=1, tiled=True),
            lax.all_gather(other_piece, "tensor", axis=1, tiled=True),
        )
        half_low, half_high = both_halves(own_half, other_half, pair_side)
        low_values = half_low.astype(jnp.float32)
        high_values = half_high.astype(jnp.float32)
        mean_square = (
            jnp.sum(low_values * low_values, axis=1) + jnp.sum(high_values * high_values, axis=1)
        ) / full_width
        row_scale = lax.rsqrt(mean_square + epsilon)[:, None]
        normed_low = (low_values * row_scale * gain_low).astype(jnp.bfloat16)
        normed_high = (high_values * row_scale * gain_high).astype(jnp.bfloat16)
        unit_adapter = lax.dynamic_index_in_dim(token_adapter, unit_slot, 0, keepdims=False)
        keep_mask = slot_of_column == unit_adapter[:, None]
        projected = lax.cond(
            active,
            lambda: product(normed_low, down_low) + product(normed_high, down_high),
            lambda: zero_rank,
        )
        kept_rank = jnp.where(keep_mask, projected, 0.0).astype(jnp.bfloat16)

        def compute():
            frozen_out = product(normed_low, weight_low) + product(normed_high, weight_high)
            adapted = product(kept_rank, up_own)
            return (own_piece.astype(jnp.float32) + frozen_out + adapted).astype(jnp.bfloat16)

        fresh_piece = lax.cond(active, compute, lambda: zero_piece)
        previous = lax.dynamic_slice_in_dim(results, unit_slot * unit_rows, unit_rows, 0)
        results = lax.dynamic_update_slice_in_dim(
            results, jnp.where(active, fresh_piece, previous), unit_slot * unit_rows, 0
        )
        moved_piece = shifted(fresh_piece, "section", 2)
        return (moved_piece, incoming_other, results)

    carry = lax.fori_loop(0, unit_count + levels - 1, pipe_step, (zero_piece, zero_piece, results))
    return carry[2][None]


def solution(mesh):
    return jax.shard_map(
        local,
        mesh=mesh,
        in_specs=(
            P(None, "tensor"),
            P(),
            P(),
            P(),
            P("section"),
            P("section", None, "tensor"),
            P("section", None),
            P("section", "tensor", None, None),
            P("section", "tensor", None, None),
        ),
        out_specs=P("section", None, "tensor"),
        check_vma=False,
    )
```

profile of v0, /device:TPU:28, one launch (start us, length us, event | category | flops | bytes accessed | tf_op | source)
XLA Modules:
  0.0 410.3 jit_solution(12662796035329693665)
XLA Ops:
  7.2 2.3 select_bitcast_fusion.1
  9.5 2.3 select_bitcast_fusion
  14.1 20.4 %all-reduce.3.cloned.1.call-done = (bf16[4096,128]{1,0:T(8,128)(2,1)}, bf16[128,4096]{1,0:T(8,128)(2,1)}) async-done(((bf16[4096,128]{1,0:T(8,128)(2,1)}, bf16[128,4096]{1,0:T(8,128)(2,1)}), (bf16[4096,128]{1,0:T(8,128)(2,1)}, bf16[128,4096]{1,0:T(8,128)(2,1)})) %all-reduce.3.cloned.1.call-update) | async-done | bytes 2097168 | tf_op jit(solution)/shard_map/psum | solution.py:14
  36.0 23.6 %fusion.12 = (bf16[2,1,2048,2048]{3,2,1,0:T(8,128)(2,1)}, bf16[2,1,2048,2048]{3,2,1,0:T(8,128)(2,1)}) fusion(bf16[2,2,2048,2048]{3,2,1,0:T(8,128)(2,1)} %bitcast.42), kind=kLoop, calls=%fused_computation.40 | loop fusion | bytes 67108864 | tf_op jit(solution)/shard_map/slice | solution.py:62
  63.5 339.9 %while.19 = (s32[]{:T(128)}, bf16[32,2048]{1,0:T(8,128)(2,1)S(1)}, bf16[128,2048]{1,0:T(8,128)(2,1)}, s32[]{:T(128)}, pred[]{:T(512)}, /*index=5*/pred[]{:T(512)...) while((s32[]{:T(128)}, bf16[32,2048]{1,0:T(8,128)(2,1)S(1)}, ...), condition=%wide.region_11.12_spmd.clone, body=%wide.region_4.11_spmd.clone.sunk | while | flops 1160463360 | bytes 109939448 | solution.py:128
  68.0 2.1 collective-permute-done
  76.3 4.5 %collective-permute-done.1 = bf16[32,2048]{1,0:T(8,128)(2,1)S(1)} collective-permute-done((bf16[32,2048]{1,0:T(8,128)(2,1)S(1)}, bf16[32,2048]{1,0:T(8,128)(2,1)S(1)}, u32[]{:S(2)}, u32[]{:S(2)}) %collective-permute-start.1) | collective-permute-done | bytes 131104 | tf_op jit(solution)/shard_map/while/body/eval_jaxpr/ppermute | solution.py:26
  93.1 4.5 %collective-permute-done.1 = bf16[32,2048]{1,0:T(8,128)(2,1)S(1)} collective-permute-done((bf16[32,2048]{1,0:T(8,128)(2,1)S(1)}, bf16[32,2048]{1,0:T(8,128)(2,1)S(1)}, u32[]{:S(2)}, u32[]{:S(2)}) %collective-permute-start.1) | collective-permute-done | bytes 131104 | tf_op jit(solution)/shard_map/while/body/eval_jaxpr/ppermute | solution.py:26
  110.0 5.2 %collective-permute-done.1 = bf16[32,2048]{1,0:T(8,128)(2,1)S(1)} collective-permute-done((bf16[32,2048]{1,0:T(8,128)(2,1)S(1)}, bf16[32,2048]{1,0:T(8,128)(2,1)S(1)}, u32[]{:S(2)}, u32[]{:S(2)}) %collective-permute-start.1) | collective-permute-done | bytes 131104 | tf_op jit(solution)/shard_map/while/body/eval_jaxpr/ppermute | solution.py:26
  127.4 5.4 %collective-permute-done.1 = bf16[32,2048]{1,0:T(8,128)(2,1)S(1)} collective-permute-done((bf16[32,2048]{1,0:T(8,128)(2,1)S(1)}, bf16[32,2048]{1,0:T(8,128)(2,1)S(1)}, u32[]{:S(2)}, u32[]{:S(2)}) %collective-permute-start.1) | collective-permute-done | bytes 131104 | tf_op jit(solution)/shard_map/while/body/eval_jaxpr/ppermute | solution.py:26
  145.2 5.4 %collective-permute-done.1 = bf16[32,2048]{1,0:T(8,128)(2,1)S(1)} collective-permute-done((bf16[32,2048]{1,0:T(8,128)(2,1)S(1)}, bf16[32,2048]{1,0:T(8,128)(2,1)S(1)}, u32[]{:S(2)}, u32[]{:S(2)}) %collective-permute-start.1) | collective-permute-done | bytes 131104 | tf_op jit(solution)/shard_map/while/body/eval_jaxpr/ppermute | solution.py:26
  162.9 5.4 %collective-permute-done.1 = bf16[32,2048]{1,0:T(8,128)(2,1)S(1)} collective-permute-done((bf16[32,2048]{1,0:T(8,128)(2,1)S(1)}, bf16[32,2048]{1,0:T(8,128)(2,1)S(1)}, u32[]{:S(2)}, u32[]{:S(2)}) %collective-permute-start.1) | collective-permute-done | bytes 131104 | tf_op jit(solution)/shard_map/while/body/eval_jaxpr/ppermute | solution.py:26
  180.6 95.4 %collective-permute-done.1 = bf16[32,2048]{1,0:T(8,128)(2,1)S(1)} collective-permute-done((bf16[32,2048]{1,0:T(8,128)(2,1)S(1)}, bf16[32,2048]{1,0:T(8,128)(2,1)S(1)}, u32[]{:S(2)}, u32[]{:S(2)}) %collective-permute-start.1) | collective-permute-done | bytes 131104 | tf_op jit(solution)/shard_map/while/body/eval_jaxpr/ppermute | solution.py:26
  286.0 13.8 %conditional.7 = (bf16[32,2048]{1,0:T(8,128)(2,1)S(1)}) conditional(s32[]{:T(128)} %convert_element_type.109, () %tuple.71, (bf16[32,2048]{1,0:T(8,128)(2,1)S(1)}, bf16[32,4096]{1,0:T(8,128)(2,1)S(1)}, bf16[4096,2048]{1,0:T(8,128)(2,1)}, bf16[32,4096]{1,0:T(8,128)(2,1)S(1)}, bf16[4096,2048]{1,0:T(8,128)(2,1)}, ...), branch_computations={%region_9.9_spmd, %region_10.10_spmd} | conditional | flops 1090846720 | bytes 103030816 | solution.py:120
  286.0 8.9 %fusion.14 = f32[32,2048]{1,0:T(8,128)S(1)} fusion(bf16[32,4096]{1,0:T(8,128)(2,1)S(1)} %get-tuple-element.457, bf16[4096,2048]{1,0:T(8,128)(2,1)} %get-tuple-element.458), kind=kOutput, calls=%fused_computation.42 | convolution fusion | flops 536870912 | bytes 17301504 | tf_op jit(solution)/shard_map/while/body/eval_jaxpr/cond/branch_1_fun/dot_general | solution.py:30
  296.5 3.0 fusion.2
  302.7 5.4 %collective-permute-done.1 = bf16[32,2048]{1,0:T(8,128)(2,1)S(1)} collective-permute-done((bf16[32,2048]{1,0:T(8,128)(2,1)S(1)}, bf16[32,2048]{1,0:T(8,128)(2,1)S(1)}, u32[]{:S(2)}, u32[]{:S(2)}) %collective-permute-start.1) | collective-permute-done | bytes 131104 | tf_op jit(solution)/shard_map/while/body/eval_jaxpr/ppermute | solution.py:26
  312.1 2.1 collective-permute-done
  318.0 13.8 %conditional.7 = (bf16[32,2048]{1,0:T(8,128)(2,1)S(1)}) conditional(s32[]{:T(128)} %convert_element_type.109, () %tuple.71, (bf16[32,2048]{1,0:T(8,128)(2,1)S(1)}, bf16[32,4096]{1,0:T(8,128)(2,1)S(1)}, bf16[4096,2048]{1,0:T(8,128)(2,1)}, bf16[32,4096]{1,0:T(8,128)(2,1)S(1)}, bf16[4096,2048]{1,0:T(8,128)(2,1)}, ...), branch_computations={%region_9.9_spmd, %region_10.10_spmd} | conditional | flops 1090846720 | bytes 103030816 | solution.py:120
  318.0 8.9 %fusion.14 = f32[32,2048]{1,0:T(8,128)S(1)} fusion(bf16[32,4096]{1,0:T(8,128)(2,1)S(1)} %get-tuple-element.457, bf16[4096,2048]{1,0:T(8,128)(2,1)} %get-tuple-element.458), kind=kOutput, calls=%fused_computation.42 | convolution fusion | flops 536870912 | bytes 17301504 | tf_op jit(solution)/shard_map/while/body/eval_jaxpr/cond/branch_1_fun/dot_general | solution.py:30
  328.6 3.0 fusion.2
  334.7 5.4 %collective-permute-done.1 = bf16[32,2048]{1,0:T(8,128)(2,1)S(1)} collective-permute-done((bf16[32,2048]{1,0:T(8,128)(2,1)S(1)}, bf16[32,2048]{1,0:T(8,128)(2,1)S(1)}, u32[]{:S(2)}, u32[]{:S(2)}) %collective-permute-start.1) | collective-permute-done | bytes 131104 | tf_op jit(solution)/shard_map/while/body/eval_jaxpr/ppermute | solution.py:26
  344.2 2.1 collective-permute-done
  350.1 13.8 %conditional.7 = (bf16[32,2048]{1,0:T(8,128)(2,1)S(1)}) conditional(s32[]{:T(128)} %convert_element_type.109, () %tuple.71, (bf16[32,2048]{1,0:T(8,128)(2,1)S(1)}, bf16[32,4096]{1,0:T(8,128)(2,1)S(1)}, bf16[4096,2048]{1,0:T(8,128)(2,1)}, bf16[32,4096]{1,0:T(8,128)(2,1)S(1)}, bf16[4096,2048]{1,0:T(8,128)(2,1)}, ...), branch_computations={%region_9.9_spmd, %region_10.10_spmd} | conditional | flops 1090846720 | bytes 103030816 | solution.py:120
  350.1 8.9 %fusion.14 = f32[32,2048]{1,0:T(8,128)S(1)} fusion(bf16[32,4096]{1,0:T(8,128)(2,1)S(1)} %get-tuple-element.457, bf16[4096,2048]{1,0:T(8,128)(2,1)} %get-tuple-element.458), kind=kOutput, calls=%fused_computation.42 | convolution fusion | flops 536870912 | bytes 17301504 | tf_op jit(solution)/shard_map/while/body/eval_jaxpr/cond/branch_1_fun/dot_general | solution.py:30
  360.6 3.0 fusion.2
  366.8 5.4 %collective-permute-done.1 = bf16[32,2048]{1,0:T(8,128)(2,1)S(1)} collective-permute-done((bf16[32,2048]{1,0:T(8,128)(2,1)S(1)}, bf16[32,2048]{1,0:T(8,128)(2,1)S(1)}, u32[]{:S(2)}, u32[]{:S(2)}) %collective-permute-start.1) | collective-permute-done | bytes 131104 | tf_op jit(solution)/shard_map/while/body/eval_jaxpr/ppermute | solution.py:26
  376.2 2.1 collective-permute-done
  382.2 13.8 %conditional.7 = (bf16[32,2048]{1,0:T(8,128)(2,1)S(1)}) conditional(s32[]{:T(128)} %convert_element_type.109, () %tuple.71, (bf16[32,2048]{1,0:T(8,128)(2,1)S(1)}, bf16[32,4096]{1,0:T(8,128)(2,1)S(1)}, bf16[4096,2048]{1,0:T(8,128)(2,1)}, bf16[32,4096]{1,0:T(8,128)(2,1)S(1)}, bf16[4096,2048]{1,0:T(8,128)(2,1)}, ...), branch_computations={%region_9.9_spmd, %region_10.10_spmd} | conditional | flops 1090846720 | bytes 103030816 | solution.py:120
  382.2 8.9 %fusion.14 = f32[32,2048]{1,0:T(8,128)S(1)} fusion(bf16[32,4096]{1,0:T(8,128)(2,1)S(1)} %get-tuple-element.457, bf16[4096,2048]{1,0:T(8,128)(2,1)} %get-tuple-element.458), kind=kOutput, calls=%fused_computation.42 | convolution fusion | flops 536870912 | bytes 17301504 | tf_op jit(solution)/shard_map/while/body/eval_jaxpr/cond/branch_1_fun/dot_general | solution.py:30
  392.7 3.0 fusion.2
  398.9 4.5 %collective-permute-done.1 = bf16[32,2048]{1,0:T(8,128)(2,1)S(1)} collective-permute-done((bf16[32,2048]{1,0:T(8,128)(2,1)S(1)}, bf16[32,2048]{1,0:T(8,128)(2,1)S(1)}, u32[]{:S(2)}, u32[]{:S(2)}) %collective-permute-start.1) | collective-permute-done | bytes 131104 | tf_op jit(solution)/shard_map/while/body/eval_jaxpr/ppermute | solution.py:26
  (213 shorter events, 146.7 us)
Async XLA Ops:
  6.5 28.0 %all-reduce.3.cloned.1.call-start = ((), (), s32[]{:S(2)}) async-start(), calls=%async_computation | async-start | bytes 4194304 | tf_op jit(solution)/shard_map/psum | solution.py:14
  12.6 47.7 %collective-permute-start.2 = (bf16[4096]{0:T(1024)(128)(2,1)S(1)}, bf16[4096]{0:T(1024)(128)(2,1)S(1)}, u32[]{:S(2)}, u32[]{:S(2)}) collective-permute-start(bf16[4096]{0:T(1024)(128)(2,1)S(1)} %reduce), channel_id=1, source_target_pairs={{0,2},{2,0},{4,6},{6,4},{8,10},{10,8},{12,14},{14,12},{16,18},{18,... | collective-permute-start | bytes 24584 | tf_op jit(solution)/shard_map/ppermute | solution.py:20
  34.6 26.4 %collective-permute-start.3 = (bf16[4096,128]{1,0:T(8,128)(2,1)}, bf16[4096,128]{1,0:T(8,128)(2,1)}, u32[]{:S(2)}, u32[]{:S(2)}) collective-permute-start(bf16[4096,128]{1,0:T(8,128)(2,1)} %get-tuple-element.551), channel_id=1, source_target_pairs={{0,2},{2,0},{4,6},{6,4},{8,10},{10,8},{12,14},{14,12},{16,18},{18,... | collective-permute-start | bytes 3145736 | tf_op jit(solution)/shard_map/ppermute | solution.py:20
  36.0 23.6 %copy-start.2 = (s32[4,8]{1,0:T(4,128)S(1)}, s32[4,8]{1,0:T(4,128)}, u32[]{:S(2)}) copy-start(s32[4,8]{1,0:T(4,128)} %param.17) | copy-start | bytes 388
  36.0 23.6 %copy-start.3 = (s32[4,32]{1,0:T(4,128)S(1)}, s32[4,32]{1,0:T(4,128)}, u32[]{:S(2)}) copy-start(s32[4,32]{1,0:T(4,128)} %param.16) | copy-start | bytes 1540
  36.0 23.7 %copy-start.4 = (s32[6]{0:T(128)S(1)}, s32[6]{0:T(128)}, u32[]{:S(2)}) copy-start(s32[6]{0:T(128)} %param.18) | copy-start | bytes 76
  36.0 24.9 %copy-start.1 = (bf16[128,4096]{1,0:T(8,128)(2,1)S(1)}, bf16[128,4096]{1,0:T(8,128)(2,1)}, u32[]{:S(2)}) copy-start(bf16[128,4096]{1,0:T(8,128)(2,1)} %get-tuple-element.552) | copy-start | bytes 3145732
  64.6 5.5 %collective-permute-start = (bf16[32,2048]{1,0:T(8,128)(2,1)S(1)}, bf16[32,2048]{1,0:T(8,128)(2,1)S(1)}, u32[]{:S(2)}, u32[]{:S(2)}) collective-permute-start(bf16[32,2048]{1,0:T(8,128)(2,1)S(1)} %dynamic-slice_select_fusion.2), channel_id=1, source_target_pairs={{0,2},{2,0},{4,6},{6,4},{8,10},{10,8},{12,14},{14,12},{16,18},{18,... | collective-permute-start | bytes 393224 | tf_op jit(solution)/shard_map/while/body/eval_jaxpr/ppermute | solution.py:20
  73.4 7.4 %collective-permute-start.1 = (bf16[32,2048]{1,0:T(8,128)(2,1)S(1)}, bf16[32,2048]{1,0:T(8,128)(2,1)S(1)}, u32[]{:S(2)}, u32[]{:S(2)}) collective-permute-start(bf16[32,2048]{1,0:T(8,128)(2,1)S(1)} %get-tuple-element.738), channel_id=1, source_target_pairs={{0,4},{2,6},{4,8},{6,10},{8,12},{10,14},{12,16},{14,18},{16,20},{1... | collective-permute-start | bytes 393224 | tf_op jit(solution)/shard_map/while/body/eval_jaxpr/ppermute | solution.py:26
  81.9 5.0 %collective-permute-start = (bf16[32,2048]{1,0:T(8,128)(2,1)S(1)}, bf16[32,2048]{1,0:T(8,128)(2,1)S(1)}, u32[]{:S(2)}, u32[]{:S(2)}) collective-permute-start(bf16[32,2048]{1,0:T(8,128)(2,1)S(1)} %dynamic-slice_select_fusion.2), channel_id=1, source_target_pairs={{0,2},{2,0},{4,6},{6,4},{8,10},{10,8},{12,14},{14,12},{16,18},{18,... | collective-permute-start | bytes 393224 | tf_op jit(solution)/shard_map/while/body/eval_jaxpr/ppermute | solution.py:20
  90.2 7.4 %collective-permute-start.1 = (bf16[32,2048]{1,0:T(8,128)(2,1)S(1)}, bf16[32,2048]{1,0:T(8,128)(2,1)S(1)}, u32[]{:S(2)}, u32[]{:S(2)}) collective-permute-start(bf16[32,2048]{1,0:T(8,128)(2,1)S(1)} %get-tuple-element.738), channel_id=1, source_target_pairs={{0,4},{2,6},{4,8},{6,10},{8,12},{10,14},{12,16},{14,18},{16,20},{1... | collective-permute-start | bytes 393224 | tf_op jit(solution)/shard_map/while/body/eval_jaxpr/ppermute | solution.py:26
  98.7 5.0 %collective-permute-start = (bf16[32,2048]{1,0:T(8,128)(2,1)S(1)}, bf16[32,2048]{1,0:T(8,128)(2,1)S(1)}, u32[]{:S(2)}, u32[]{:S(2)}) collective-permute-start(bf16[32,2048]{1,0:T(8,128)(2,1)S(1)} %dynamic-slice_select_fusion.2), channel_id=1, source_target_pairs={{0,2},{2,0},{4,6},{6,4},{8,10},{10,8},{12,14},{14,12},{16,18},{18,... | collective-permute-start | bytes 393224 | tf_op jit(solution)/shard_map/while/body/eval_jaxpr/ppermute | solution.py:20
  107.1 8.1 %collective-permute-start.1 = (bf16[32,2048]{1,0:T(8,128)(2,1)S(1)}, bf16[32,2048]{1,0:T(8,128)(2,1)S(1)}, u32[]{:S(2)}, u32[]{:S(2)}) collective-permute-start(bf16[32,2048]{1,0:T(8,128)(2,1)S(1)} %get-tuple-element.738), channel_id=1, source_target_pairs={{0,4},{2,6},{4,8},{6,10},{8,12},{10,14},{12,16},{14,18},{16,20},{1... | collective-permute-start | bytes 393224 | tf_op jit(solution)/shard_map/while/body/eval_jaxpr/ppermute | solution.py:26
  116.2 5.0 %collective-permute-start = (bf16[32,2048]{1,0:T(8,128)(2,1)S(1)}, bf16[32,2048]{1,0:T(8,128)(2,1)S(1)}, u32[]{:S(2)}, u32[]{:S(2)}) collective-permute-start(bf16[32,2048]{1,0:T(8,128)(2,1)S(1)} %dynamic-slice_select_fusion.2), channel_id=1, source_target_pairs={{0,2},{2,0},{4,6},{6,4},{8,10},{10,8},{12,14},{14,12},{16,18},{18,... | collective-permute-start | bytes 393224 | tf_op jit(solution)/shard_map/while/body/eval_jaxpr/ppermute | solution.py:20
  124.5 8.3 %collective-permute-start.1 = (bf16[32,2048]{1,0:T(8,128)(2,1)S(1)}, bf16[32,2048]{1,0:T(8,128)(2,1)S(1)}, u32[]{:S(2)}, u32[]{:S(2)}) collective-permute-start(bf16[32,2048]{1,0:T(8,128)(2,1)S(1)} %get-tuple-element.738), channel_id=1, source_target_pairs={{0,4},{2,6},{4,8},{6,10},{8,12},{10,14},{12,16},{14,18},{16,20},{1... | collective-permute-start | bytes 393224 | tf_op jit(solution)/shard_map/while/body/eval_jaxpr/ppermute | solution.py:26
  133.9 5.0 %collective-permute-start = (bf16[32,2048]{1,0:T(8,128)(2,1)S(1)}, bf16[32,2048]{1,0:T(8,128)(2,1)S(1)}, u32[]{:S(2)}, u32[]{:S(2)}) collective-permute-start(bf16[32,2048]{1,0:T(8,128)(2,1)S(1)} %dynamic-slice_select_fusion.2), channel_id=1, source_target_pairs={{0,2},{2,0},{4,6},{6,4},{8,10},{10,8},{12,14},{14,12},{16,18},{18,... | collective-permute-start | bytes 393224 | tf_op jit(solution)/shard_map/while/body/eval_jaxpr/ppermute | solution.py:20
  142.3 8.3 %collective-permute-start.1 = (bf16[32,2048]{1,0:T(8,128)(2,1)S(1)}, bf16[32,2048]{1,0:T(8,128)(2,1)S(1)}, u32[]{:S(2)}, u32[]{:S(2)}) collective-permute-start(bf16[32,2048]{1,0:T(8,128)(2,1)S(1)} %get-tuple-element.738), channel_id=1, source_target_pairs={{0,4},{2,6},{4,8},{6,10},{8,12},{10,14},{12,16},{14,18},{16,20},{1... | collective-permute-start | bytes 393224 | tf_op jit(solution)/shard_map/while/body/eval_jaxpr/ppermute | solution.py:26
  151.6 5.0 %collective-permute-start = (bf16[32,2048]{1,0:T(8,128)(2,1)S(1)}, bf16[32,2048]{1,0:T(8,128)(2,1)S(1)}, u32[]{:S(2)}, u32[]{:S(2)}) collective-permute-start(bf16[32,2048]{1,0:T(8,128)(2,1)S(1)} %dynamic-slice_select_fusion.2), channel_id=1, source_target_pairs={{0,2},{2,0},{4,6},{6,4},{8,10},{10,8},{12,14},{14,12},{16,18},{18,... | collective-permute-start | bytes 393224 | tf_op jit(solution)/shard_map/while/body/eval_jaxpr/ppermute | solution.py:20
  160.0 8.3 %collective-permute-start.1 = (bf16[32,2048]{1,0:T(8,128)(2,1)S(1)}, bf16[32,2048]{1,0:T(8,128)(2,1)S(1)}, u32[]{:S(2)}, u32[]{:S(2)}) collective-permute-start(bf16[32,2048]{1,0:T(8,128)(2,1)S(1)} %get-tuple-element.738), channel_id=1, source_target_pairs={{0,4},{2,6},{4,8},{6,10},{8,12},{10,14},{12,16},{14,18},{16,20},{1... | collective-permute-start | bytes 393224 | tf_op jit(solution)/shard_map/while/body/eval_jaxpr/ppermute | solution.py:26
  169.3 5.0 %collective-permute-start = (bf16[32,2048]{1,0:T(8,128)(2,1)S(1)}, bf16[32,2048]{1,0:T(8,128)(2,1)S(1)}, u32[]{:S(2)}, u32[]{:S(2)}) collective-permute-start(bf16[32,2048]{1,0:T(8,128)(2,1)S(1)} %dynamic-slice_select_fusion.2), channel_id=1, source_target_pairs={{0,2},{2,0},{4,6},{6,4},{8,10},{10,8},{12,14},{14,12},{16,18},{18,... | collective-permute-start | bytes 393224 | tf_op jit(solution)/shard_map/while/body/eval_jaxpr/ppermute | solution.py:20
  177.7 98.3 %collective-permute-start.1 = (bf16[32,2048]{1,0:T(8,128)(2,1)S(1)}, bf16[32,2048]{1,0:T(8,128)(2,1)S(1)}, u32[]{:S(2)}, u32[]{:S(2)}) collective-permute-start(bf16[32,2048]{1,0:T(8,128)(2,1)S(1)} %get-tuple-element.738), channel_id=1, source_target_pairs={{0,4},{2,6},{4,8},{6,10},{8,12},{10,14},{12,16},{14,18},{16,20},{1... | collective-permute-start | bytes 393224 | tf_op jit(solution)/shard_map/while/body/eval_jaxpr/ppermute | solution.py:26
  277.0 5.0 %collective-permute-start = (bf16[32,2048]{1,0:T(8,128)(2,1)S(1)}, bf16[32,2048]{1,0:T(8,128)(2,1)S(1)}, u32[]{:S(2)}, u32[]{:S(2)}) collective-permute-start(bf16[32,2048]{1,0:T(8,128)(2,1)S(1)} %dynamic-slice_select_fusion.2), channel_id=1, source_target_pairs={{0,2},{2,0},{4,6},{6,4},{8,10},{10,8},{12,14},{14,12},{16,18},{18,... | collective-permute-start | bytes 393224 | tf_op jit(solution)/shard_map/while/body/eval_jaxpr/ppermute | solution.py:20
  286.0 10.5 %copy-start = (bf16[4096,2048]{1,0:T(8,128)(2,1)S(1)}, bf16[4096,2048]{1,0:T(8,128)(2,1)}, u32[]{:S(2)}) copy-start(bf16[4096,2048]{1,0:T(8,128)(2,1)} %get-tuple-element.460) | copy-start | bytes 50331652 | tf_op jit(solution)/shard_map/while/body/eval_jaxpr/cond
  299.8 8.3 %collective-permute-start.1 = (bf16[32,2048]{1,0:T(8,128)(2,1)S(1)}, bf16[32,2048]{1,0:T(8,128)(2,1)S(1)}, u32[]{:S(2)}, u32[]{:S(2)}) collective-permute-start(bf16[32,2048]{1,0:T(8,128)(2,1)S(1)} %get-tuple-element.738), channel_id=1, source_target_pairs={{0,4},{2,6},{4,8},{6,10},{8,12},{10,14},{12,16},{14,18},{16,20},{1... | collective-permute-start | bytes 393224 | tf_op jit(solution)/shard_map/while/body/eval_jaxpr/ppermute | solution.py:26
  309.1 5.0 %collective-permute-start = (bf16[32,2048]{1,0:T(8,128)(2,1)S(1)}, bf16[32,2048]{1,0:T(8,128)(2,1)S(1)}, u32[]{:S(2)}, u32[]{:S(2)}) collective-permute-start(bf16[32,2048]{1,0:T(8,128)(2,1)S(1)} %dynamic-slice_select_fusion.2), channel_id=1, source_target_pairs={{0,2},{2,0},{4,6},{6,4},{8,10},{10,8},{12,14},{14,12},{16,18},{18,... | collective-permute-start | bytes 393224 | tf_op jit(solution)/shard_map/while/body/eval_jaxpr/ppermute | solution.py:20
  318.0 10.5 %copy-start = (bf16[4096,2048]{1,0:T(8,128)(2,1)S(1)}, bf16[4096,2048]{1,0:T(8,128)(2,1)}, u32[]{:S(2)}) copy-start(bf16[4096,2048]{1,0:T(8,128)(2,1)} %get-tuple-element.460) | copy-start | bytes 50331652 | tf_op jit(solution)/shard_map/while/body/eval_jaxpr/cond
  331.8 8.3 %collective-permute-start.1 = (bf16[32,2048]{1,0:T(8,128)(2,1)S(1)}, bf16[32,2048]{1,0:T(8,128)(2,1)S(1)}, u32[]{:S(2)}, u32[]{:S(2)}) collective-permute-start(bf16[32,2048]{1,0:T(8,128)(2,1)S(1)} %get-tuple-element.738), channel_id=1, source_target_pairs={{0,4},{2,6},{4,8},{6,10},{8,12},{10,14},{12,16},{14,18},{16,20},{1... | collective-permute-start | bytes 393224 | tf_op jit(solution)/shard_map/while/body/eval_jaxpr/ppermute | solution.py:26
  341.2 5.0 %collective-permute-start = (bf16[32,2048]{1,0:T(8,128)(2,1)S(1)}, bf16[32,2048]{1,0:T(8,128)(2,1)S(1)}, u32[]{:S(2)}, u32[]{:S(2)}) collective-permute-start(bf16[32,2048]{1,0:T(8,128)(2,1)S(1)} %dynamic-slice_select_fusion.2), channel_id=1, source_target_pairs={{0,2},{2,0},{4,6},{6,4},{8,10},{10,8},{12,14},{14,12},{16,18},{18,... | collective-permute-start | bytes 393224 | tf_op jit(solution)/shard_map/while/body/eval_jaxpr/ppermute | solution.py:20
  350.1 10.5 %copy-start = (bf16[4096,2048]{1,0:T(8,128)(2,1)S(1)}, bf16[4096,2048]{1,0:T(8,128)(2,1)}, u32[]{:S(2)}) copy-start(bf16[4096,2048]{1,0:T(8,128)(2,1)} %get-tuple-element.460) | copy-start | bytes 50331652 | tf_op jit(solution)/shard_map/while/body/eval_jaxpr/cond
  363.9 8.3 %collective-permute-start.1 = (bf16[32,2048]{1,0:T(8,128)(2,1)S(1)}, bf16[32,2048]{1,0:T(8,128)(2,1)S(1)}, u32[]{:S(2)}, u32[]{:S(2)}) collective-permute-start(bf16[32,2048]{1,0:T(8,128)(2,1)S(1)} %get-tuple-element.738), channel_id=1, source_target_pairs={{0,4},{2,6},{4,8},{6,10},{8,12},{10,14},{12,16},{14,18},{16,20},{1... | collective-permute-start | bytes 393224 | tf_op jit(solution)/shard_map/while/body/eval_jaxpr/ppermute | solution.py:26
  373.3 5.0 %collective-permute-start = (bf16[32,2048]{1,0:T(8,128)(2,1)S(1)}, bf16[32,2048]{1,0:T(8,128)(2,1)S(1)}, u32[]{:S(2)}, u32[]{:S(2)}) collective-permute-start(bf16[32,2048]{1,0:T(8,128)(2,1)S(1)} %dynamic-slice_select_fusion.2), channel_id=1, source_target_pairs={{0,2},{2,0},{4,6},{6,4},{8,10},{10,8},{12,14},{14,12},{16,18},{18,... | collective-permute-start | bytes 393224 | tf_op jit(solution)/shard_map/while/body/eval_jaxpr/ppermute | solution.py:20
  396.0 7.4 %collective-permute-start.1 = (bf16[32,2048]{1,0:T(8,128)(2,1)S(1)}, bf16[32,2048]{1,0:T(8,128)(2,1)S(1)}, u32[]{:S(2)}, u32[]{:S(2)}) collective-permute-start(bf16[32,2048]{1,0:T(8,128)(2,1)S(1)} %get-tuple-element.738), channel_id=1, source_target_pairs={{0,4},{2,6},{4,8},{6,10},{8,12},{10,14},{12,16},{14,18},{16,20},{1... | collective-permute-start | bytes 393224 | tf_op jit(solution)/shard_map/while/body/eval_jaxpr/ppermute | solution.py:26
  (1 other events, 10.5 us)
Sparse Core Ops, SparseCore 0:
  11.9 22.5 all-reduce.2
where the time goes:
time: 413 us; the launch traced here: 410 us
  waiting for transfers between devices  188 us (46%)
  other arithmetic  51.5 us (12%)
  matrix products  50.8 us (12%)
  blocking collectives  43.6 us (11%)
  local copies, waits for them, and re-layouts  38.1 us (9%)
  starting transfers between devices  23 us (6%)
  between operations  14.1 us (3%)
    ppermute x11, waiting for transfers between devices, shifted(): lax.ppermute(value, axis, [(source, source + steps) for source in range(f...  147 us
    dot_general x20, matrix products, product(): return jnp.dot(left, right, preferred_element_type=jnp.float32)  50.8 us
    slice x1, local copies, waits for them, and re-layouts, local(): weight_high = split_weight[:, 1].reshape(half_width, piece_cols)  23.6 us
    all_gather x11, blocking collectives, pipe_step(): lax.all_gather(other_piece, 'tensor', axis=1, tiled=True)  21.8 us
    all_gather x11, blocking collectives, pipe_step(): lax.all_gather(own_piece, 'tensor', axis=1, tiled=True)  21.8 us
    ppermute x13, waiting for transfers between devices, from_partner(): return lax.ppermute(value, axis, pairs)  21.2 us
    psum x1, waiting for transfers between devices, spread(): return lax.psum(block, axis)  20.4 us
    dynamic_update_slice x11, other arithmetic, pipe_step(): lax.dynamic_update_slice_in_dim(results, jnp.where(active, fresh_piece, p...  17.6 us
  transfers between devices with their start and end apart: 25, of which 23 were waited for; matrix products, arithmetic and copies ran while one was open for 12% of the time, Pallas kernels for 0%

commit v1 on v0

v1 whole, which is shorter than its diff:
```python
import functools
import jax
import jax.numpy as jnp
from jax import lax
from jax.experimental import pallas as pl
from jax.experimental.pallas import tpu as pltpu
from jax.sharding import PartitionSpec as P

R = 32
MESH = pl.DeviceIdType.MESH
epsilon = 1e-05


def kernel(
    sections, tensors, units, rows, piece, chunks, ranks, jobs_of,
    hidden, ids, seg_job, job_ad, owner, frozen, gain, idown, iup,
    out,
    w, xbuf, xg, outbuf, gother, dbuf, ubuf, dsel, usel, lowbuf, kept, scale,
    wsem, xsem, psem, fsend, osend, hsem, dsem, usem, isend, gsem, lsem, lsend,
):
    levels = sections // 2
    step = piece // chunks
    full = 2 * tensors * piece
    segs, jobs = jobs_of
    s = lax.axis_index("section")
    t = lax.axis_index("tensor")
    h = lax.rem(s, 2)
    level = s // 2
    other = s + 1 - 2 * h
    b = 2 * t + h

    def peer(d):
        return lax.rem(t + d, tensors)

    def cols(c):
        return pl.ds(pl.multiple_of(c * step, step), step)

    def part(k):
        return pl.ds(pl.multiple_of(k * piece, piece), piece)

    def weight(c):
        return pltpu.make_async_copy(frozen.at[0, :, cols(c)], w.at[:, cols(c)], wsem.at[c])

    def remote(src, dst, send, recv, section, tensor):
        return pltpu.make_async_remote_copy(
            src_ref=src, dst_ref=dst, send_sem=send, recv_sem=recv,
            device_id=(section, tensor), device_id_type=MESH,
        )

    def landed(ref, sem):
        pltpu.make_async_copy(ref, ref, sem).wait()

    own_down = pltpu.make_async_copy(idown.at[0, 0, part(t), :], dbuf.at[t], dsem.at[t])
    own_up = pltpu.make_async_copy(iup.at[0, 0, :, part(t)], ubuf.at[t], usem.at[t])

    @pl.when(level == 0)
    def _():
        for hh in range(2):
            for c in range(chunks):
                def read(m, _, hh=hh, c=c):
                    slot = pl.ds(c * step, step)
                    pltpu.make_async_copy(
                        hidden.at[pl.ds(pl.multiple_of(m * rows, rows), rows), pl.ds(hh * piece + c * step, step)],
                        xbuf.at[m, 2 * t + hh, :, slot],
                        xsem.at[m, hh, c],
                    ).start()
                    return 0
                lax.fori_loop(0, units, read, 0)
    own_down.start()
    own_up.start()
    for c in range(chunks):
        weight(c).start()

    barrier = pltpu.get_barrier_semaphore()

    def greet(section, tensor):
        pl.semaphore_signal(barrier, inc=1, device_id=(section, tensor), device_id_type=MESH)

    for d in range(1, tensors):
        greet(s, peer(d))
    for d in range(tensors):
        greet(other, peer(d))

    @pl.when(level > 0)
    def _():
        greet(s - 2, t)
        greet(other - 2, t)

    @pl.when(level < levels - 1)
    def _():
        greet(s + 2, t)
        greet(other + 2, t)

    ends = (level > 0).astype(jnp.int32) + (level < levels - 1).astype(jnp.int32)
    pl.semaphore_wait(barrier, 2 * tensors - 1 + 2 * ends)

    def send_down(d):
        return remote(idown.at[0, 0, part(peer(d)), :], dbuf.at[t], isend.at[0, d], dsem.at[t], s, peer(d))

    def send_up(d):
        return remote(iup.at[0, 0, :, part(peer(d))], ubuf.at[t], isend.at[1, d], usem.at[t], s, peer(d))

    send_gain = remote(gain, gother, gsem.at[0], gsem.at[1], other, t)
    send_gain.start()
    for d in range(1, tensors):
        send_down(d).start()
        send_up(d).start()

    def forward(m, c, hh, d):
        ref = xbuf.at[m, 2 * t + hh, :, cols(c)]
        return remote(ref, ref, fsend.at[m, d, hh, c], psem.at[m, t, hh, c], s, peer(d))

    def forward_chunk(m, c):
        for hh in range(2):
            landed(xbuf.at[m, 2 * t + hh, :, cols(c)], xsem.at[m, hh, c])
            for d in range(1, tensors):
                forward(m, c, hh, d).start()

    def low_to(m, side, d):
        ref = lowbuf.at[m, b]
        section = s if side == 0 else other
        return remote(ref, ref, lsend.at[m, side, d], lsem.at[m, b], section, peer(d))

    def low_part(m):
        own = xbuf[m, b].astype(jnp.float32) * gain[0:1, part(t)].astype(jnp.float32)
        lowbuf[m, b] = jnp.dot(own.astype(jnp.bfloat16), dsel[...], preferred_element_type=jnp.float32)
        for side in range(2):
            for d in range(1 - side, tensors):
                low_to(m, side, d).start()

    def send_out(m, c, side):
        section = (s if side == 0 else other) + 2
        return remote(
            outbuf.at[m, :, cols(c)], xbuf.at[m, b, :, cols(c)],
            osend.at[m, side, c], xsem.at[m, h, c], section, t,
        )

    def write_out(m):
        return pltpu.make_async_copy(
            outbuf.at[m], out.at[0, pl.ds(pl.multiple_of(m * rows, rows), rows), :], hsem.at[m]
        )

    def first(c, _):
        forward_chunk(0, c)
        return 0

    own_down.wait()
    own_up.wait()
    for d in range(1, tensors):
        landed(dbuf.at[peer(d)], dsem.at[peer(d)])
        landed(ubuf.at[peer(d)], usem.at[peer(d)])
    who = owner[0]
    down, up = dbuf[0], ubuf[0]
    for k in range(1, tensors):
        down = jnp.where(who == k, dbuf[k], down)
        up = jnp.where(who == k, ubuf[k], up)
    dsel[...] = down
    usel[...] = up
    send_gain.wait_recv()
    lax.fori_loop(0, chunks, first, 0)
    low_part(0)

    def unit(m, _):
        for d in range(1, tensors):
            for hh in range(2):
                for c in range(chunks):
                    landed(xbuf.at[m, 2 * peer(d) + hh, :, pl.ds(c * step, step)], psem.at[m, peer(d), hh, c])
        total = jnp.zeros((rows, 1), jnp.float32)
        for k in range(2 * tensors):
            where_gain = pl.ds((k // 2) * piece, piece)
            near = gain[0:1, where_gain].astype(jnp.float32)
            far = gother[0:1, where_gain].astype(jnp.float32)
            x = xbuf[m, k].astype(jnp.float32)
            total += jnp.sum(x * x, axis=1, keepdims=True)
            xg[:, k * piece : (k + 1) * piece] = (x * jnp.where(h == k % 2, near, far)).astype(jnp.bfloat16)
        scale[...] = jnp.broadcast_to(lax.rsqrt(total / full + epsilon), scale.shape)

        def chunk(c, _):
            @pl.when(m == 0)
            def _():
                weight(c).wait()

            @pl.when(m + 1 < units)
            def _():
                forward_chunk(m + 1, c)

                @pl.when(c == chunks - 1)
                def _():
                    low_part(m + 1)

            main = jnp.dot(xg[...], w[:, cols(c)], preferred_element_type=jnp.float32)

            @pl.when(c == 0)
            def _():
                for side in range(2):
                    for d in range(1 - side, tensors):
                        blk = 2 * peer(d) + (h if side == 0 else 1 - h)
                        landed(lowbuf.at[m, blk], lsem.at[m, blk])
                low = lowbuf[m, 0]
                for k in range(1, 2 * tensors):
                    low = low + lowbuf[m, k]
                low = low * scale[:, 0:1]
                seg = ids[pl.ds(m, 1), :]
                slot = jnp.zeros_like(seg)
                for g in range(segs):
                    slot = jnp.where(seg == g, job_ad[seg_job[m, g]], slot)
                column = lax.broadcasted_iota(jnp.int32, (ranks, rows), 0) // R
                hit = jnp.where(column == slot, 1.0, 0.0).astype(jnp.bfloat16)
                eye = jnp.where(
                    lax.broadcasted_iota(jnp.int32, (rows, rows), 0)
                    == lax.broadcasted_iota(jnp.int32, (rows, rows), 1), 1.0, 0.0
                ).astype(jnp.bfloat16)
                mask = lax.dot_general(eye, hit, (((1,), (1,)), ((), ())), preferred_element_type=jnp.float32)
                kept[...] = jnp.where(mask > 0.5, low, 0.0).astype(jnp.bfloat16)

            adapted = jnp.dot(kept[...], usel[:, cols(c)], preferred_element_type=jnp.float32)
            fresh = xbuf[m, b, :, cols(c)].astype(jnp.float32) + main * scale[:, 0:1] + adapted
            outbuf[m, :, cols(c)] = fresh.astype(jnp.bfloat16)

            @pl.when(level < levels - 1)
            def _():
                for side in range(2):
                    send_out(m, c, side).start()
            return 0

        lax.fori_loop(0, chunks, chunk, 0)
        write_out(m).start()
        return 0

    lax.fori_loop(0, units, unit, 0)

    send_gain.wait_send()
    for d in range(1, tensors):
        send_down(d).wait_send()
        send_up(d).wait_send()

    def drain(m, _):
        for d in range(1, tensors):
            for hh in range(2):
                for c in range(chunks):
                    forward(m, c, hh, d).wait_send()
        for side in range(2):
            for d in range(1 - side, tensors):
                low_to(m, side, d).wait_send()

        @pl.when(level < levels - 1)
        def _():
            for side in range(2):
                for c in range(chunks):
                    send_out(m, c, side).wait_send()
        write_out(m).wait()
        return 0

    lax.fori_loop(0, units, drain, 0)


def local(
    hidden_in, segment_ids, segment_job, job_adapter, owner, frozen, norm_gain, inbox_down, inbox_up
):
    tensors = lax.axis_size("tensor")
    sections = lax.axis_size("section")
    units, rows = segment_ids.shape
    depth, piece = frozen.shape[1:]
    ranks = inbox_down.shape[3]
    chunks = max(1, min(4, piece // 256))
    step = piece // chunks
    bf16, f32 = jnp.bfloat16, jnp.float32
    anywhere = pl.BlockSpec(memory_space=pl.ANY)
    smem = pl.BlockSpec(memory_space=pltpu.SMEM)
    vmem = pl.BlockSpec(memory_space=pltpu.VMEM)
    dma = pltpu.SemaphoreType.DMA
    body = functools.partial(
        kernel, sections, tensors, units, rows, piece, chunks, ranks,
        (segment_job.shape[1], job_adapter.shape[0]),
    )
    return pl.pallas_call(
        body,
        out_shape=jax.ShapeDtypeStruct((1, units * rows, piece), bf16),
        in_specs=[anywhere, vmem, smem, smem, smem, anywhere, vmem, anywhere, anywhere],
        out_specs=anywhere,
        scratch_shapes=[
            pltpu.VMEM((depth, piece), bf16),
            pltpu.VMEM((units, 2 * tensors, rows, piece), bf16),
            pltpu.VMEM((rows, depth), bf16),
            pltpu.VMEM((units, rows, piece), bf16),
            pltpu.VMEM(norm_gain.shape, bf16),
            pltpu.VMEM((tensors, piece, ranks), bf16),
            pltpu.VMEM((tensors, ranks, piece), bf16),
            pltpu.VMEM((piece, ranks), bf16),
            pltpu.VMEM((ranks, piece), bf16),
            pltpu.VMEM((units, 2 * tensors, rows, ranks), f32),
            pltpu.VMEM((rows, ranks), bf16),
            pltpu.VMEM((rows, 128), f32),
            dma((chunks,)),
            dma((units, 2, chunks)),
            dma((units, tensors, 2, chunks)),
            dma((units, tensors, 2, chunks)),
            dma((units, 2, chunks)),
            dma((units,)),
            dma((tensors,)),
            dma((tensors,)),
            dma((2, tensors)),
            dma((2,)),
            dma((units, 2 * tensors)),
            dma((units, 2, tensors)),
        ],
        compiler_params=pltpu.CompilerParams(
            collective_id=0, has_side_effects=True, vmem_limit_bytes=60 * 2**20
        ),
    )(hidden_in, segment_ids, segment_job, job_adapter, owner, frozen, norm_gain, inbox_down, inbox_up)


def solution(mesh):
    return jax.shard_map(
        local,
        mesh=mesh,
        in_specs=(
            P(None, "tensor"),
            P(),
            P(),
            P(),
            P("section"),
            P("section", None, "tensor"),
            P("section", None),
            P("section", "tensor", None, None),
            P("section", "tensor", None, None),
        ),
        out_specs=P("section", None, "tensor"),
        check_vma=False,
    )
```

time: 413 us -> 138 us (0.33)
  waiting for transfers between devices: 188 us -> 0 us
  Pallas kernels: 0 us -> 136 us
  other arithmetic: 51.5 us -> 0 us
  matrix products: 50.8 us -> 0 us
  blocking collectives: 43.6 us -> 0 us
  local copies, waits for them, and re-layouts: 38.1 us -> 1.88 us
  starting transfers between devices: 23 us -> 0 us
  between operations: 14.1 us -> 0.66 us
    ppermute x24 -> x0, waiting for transfers between devices: 168 us -> none  [the longest x11 147 us: shifted(): lax.ppermute(value, axis, [(source, source + steps) for source in range(f...]
    pallas_call x0 -> x1, Pallas kernels: none -> 136 us  [local(): pl.pallas_call(body, out_shape=jax.ShapeDtypeStruct((1, units * rows, pie...]
    dot_general x20 -> x0, matrix products: 50.8 us -> none  [product(): return jnp.dot(left, right, preferred_element_type=jnp.float32)]
    all_gather x22 -> x0, blocking collectives: 43.6 us -> none  [the longest x11 21.8 us: pipe_step(): lax.all_gather(other_piece, 'tensor', axis=1, tiled=True)]
    slice x1 -> x0, local copies, waits for them, and re-layouts: 23.6 us -> none  [local(): weight_high = split_weight[:, 1].reshape(half_width, piece_cols)]
    ppermute x24 -> x0, starting transfers between devices: 23 us -> none  [the longest x11 14.2 us: shifted(): lax.ppermute(value, axis, [(source, source + steps) for source in range(f...]
    psum x1 -> x0, waiting for transfers between devices: 20.4 us -> none  [spread(): return lax.psum(block, axis)]
    dynamic_update_slice x11 -> x0, other arithmetic: 17.6 us -> none  [pipe_step(): lax.dynamic_update_slice_in_dim(results, jnp.where(active, fresh_piece, p...]
  transfers between devices with their start and end apart: 25 -> 0, of which waited for: 23 -> 0; matrix products, arithmetic and copies ran while one was open for 12% -> 0% of each run, Pallas kernels for 0% -> 0%
where the time goes in v1:
time: 138 us
  Pallas kernels  136 us (99%)
  local copies, waits for them, and re-layouts  1.88 us (1%)
    pallas_call x1, Pallas kernels, local(): pl.pallas_call(body, out_shape=jax.ShapeDtypeStruct((1, units * rows, pie...  136 us

profile of v1, /device:TPU:28, one launch (start us, length us, event | category | flops | bytes accessed | tf_op | source)
XLA Modules:
  0.0 138.1 jit_solution(12754616450487210751)
XLA Ops:
  0.7 135.5 %shard_map.91 = bf16[1,128,2048]{2,1,0:T(8,128)(2,1)} custom-call(bf16[128,4096]{1,0:T(8,128)(2,1)} %hidden.1, s32[4,32]{1,0:T(4,128)} %ids.1, s32[4,8]{1,0:T(4,128)} %seg_job.1, s32[6]{0:T(128)} %job_ad.1, s32[1]{0:T(128)S(6)} %copy.11.owner, bf16[1,8192,2048]{2,1,0:T(8,128)(2,1)} %frozen.1, bf16[1,4096]{1,0:T(2,128)(2,1)} %gain.1, ...), custom_call_target="tpu_custom_call" | custom-call | tf_op jit(solution)/shard_map/pallas_call | solution.py:276
  136.2 1.9 %copy.12 = bf16[1,128,2048]{2,1,0:T(8,128)(2,1)} copy(bf16[1,128,2048]{2,1,0:T(8,128)(2,1)} %shard_map.91) | data formatting | bytes 1048576

commit v2 on v1

--- a/solution.py
+++ b/solution.py
@@ -15,8 +15,8 @@
     sections, tensors, units, rows, piece, chunks, ranks, jobs_of,
     hidden, ids, seg_job, job_ad, owner, frozen, gain, idown, iup,
     out,
-    w, xbuf, xg, outbuf, gother, dbuf, ubuf, dsel, usel, lowbuf, kept, scale,
-    wsem, xsem, psem, fsend, osend, hsem, dsem, usem, isend, gsem, lsem, lsend,
+    w, xbuf, xg, acc, outbuf, gother, dbuf, ubuf, dsel, usel, lowbuf, kept, square, scale,
+    wsem, vsem, xsem, psem, fsend, osend, hsem, dsem, usem, isend, gsem, lsem, lsend,
 ):
     levels = sections // 2
     step = piece // chunks
@@ -38,8 +38,19 @@
     def part(k):
         return pl.ds(pl.multiple_of(k * piece, piece), piece)
 
-    def weight(c):
-        return pltpu.make_async_copy(frozen.at[0, :, cols(c)], w.at[:, cols(c)], wsem.at[c])
+    def near_rows(hh, c):
+        return pl.ds(pl.multiple_of((2 * t + hh) * piece + c * step, step), step)
+
+    def far_rows(d):
+        return pl.ds(pl.multiple_of(2 * peer(d) * piece, piece), 2 * piece)
+
+    def near_weight(hh, c):
+        return pltpu.make_async_copy(frozen.at[0, near_rows(hh, c), :], w.at[near_rows(hh, c), :], wsem.at[hh, c])
+
+    def far_weight(d, c):
+        return pltpu.make_async_copy(
+            frozen.at[0, far_rows(d), cols(c)], w.at[far_rows(d), cols(c)], vsem.at[d, c]
+        )
 
     def remote(src, dst, send, recv, section, tensor):
         return pltpu.make_async_remote_copy(
@@ -69,7 +80,11 @@
     own_down.start()
     own_up.start()
     for c in range(chunks):
-        weight(c).start()
+        for hh in range(2):
+            near_weight(hh, c).start()
+    for c in range(chunks):
+        for d in range(1, tensors):
+            far_weight(d, c).start()
 
     barrier = pltpu.get_barrier_semaphore()
 
@@ -110,11 +125,10 @@
         ref = xbuf.at[m, 2 * t + hh, :, cols(c)]
         return remote(ref, ref, fsend.at[m, d, hh, c], psem.at[m, t, hh, c], s, peer(d))
 
-    def forward_chunk(m, c):
-        for hh in range(2):
-            landed(xbuf.at[m, 2 * t + hh, :, cols(c)], xsem.at[m, hh, c])
-            for d in range(1, tensors):
-                forward(m, c, hh, d).start()
+    def forward_one(m, c, hh):
+        landed(xbuf.at[m, 2 * t + hh, :, cols(c)], xsem.at[m, hh, c])
+        for d in range(1, tensors):
+            forward(m, c, hh, d).start()
 
     def low_to(m, side, d):
         ref = lowbuf.at[m, b]
@@ -140,9 +154,19 @@
             outbuf.at[m], out.at[0, pl.ds(pl.multiple_of(m * rows, rows), rows), :], hsem.at[m]
         )
 
-    def first(c, _):
-        forward_chunk(0, c)
-        return 0
+    def forward_chunk(m, c):
+        forward_one(m, c, h)
+
+        @pl.when(c == chunks - 1)
+        def _():
+            low_part(m)
+
+        forward_one(m, c, 1 - h)
+
+    def gained(x, k_side, where_gain):
+        near = gain[0:1, where_gain].astype(jnp.float32)
+        far = gother[0:1, where_gain].astype(jnp.float32)
+        return (x * jnp.where(h == k_side, near, far)).astype(jnp.bfloat16)
 
     own_down.wait()
     own_up.wait()
@@ -157,38 +181,54 @@
     dsel[...] = down
     usel[...] = up
     send_gain.wait_recv()
-    lax.fori_loop(0, chunks, first, 0)
-    low_part(0)
 
     def unit(m, _):
+        square[...] = jnp.zeros_like(square)
+        acc[...] = jnp.zeros_like(acc)
+        forward_chunk(m, 0)
+
+        def near(c, _):
+            @pl.when(c + 1 < chunks)
+            def _():
+                forward_chunk(m, c + 1)
+
+            @pl.when(m == 0)
+            def _():
+                for hh in range(2):
+                    near_weight(hh, c).wait()
+
+            part_sum = acc[...]
+            total = jnp.zeros((rows, 1), jnp.float32)
+            for hh in range(2):
+                x = xbuf[m, 2 * t + hh, :, cols(c)].astype(jnp.float32)
+                total += jnp.sum(x * x, axis=1, keepdims=True)
+                values = gained(x, hh, pl.ds(pl.multiple_of(t * piece + c * step, step), step))
+                part_sum += jnp.dot(values, w[near_rows(hh, c), :], preferred_element_type=jnp.float32)
+            acc[...] = part_sum
+            square[...] += jnp.broadcast_to(total, square.shape)
+            return 0
+
+        lax.fori_loop(0, chunks, near, 0)
+
+        total = square[:, 0:1]
         for d in range(1, tensors):
             for hh in range(2):
                 for c in range(chunks):
                     landed(xbuf.at[m, 2 * peer(d) + hh, :, pl.ds(c * step, step)], psem.at[m, peer(d), hh, c])
-        total = jnp.zeros((rows, 1), jnp.float32)
-        for k in range(2 * tensors):
-            where_gain = pl.ds((k // 2) * piece, piece)
-            near = gain[0:1, where_gain].astype(jnp.float32)
-            far = gother[0:1, where_gain].astype(jnp.float32)
-            x = xbuf[m, k].astype(jnp.float32)
-            total += jnp.sum(x * x, axis=1, keepdims=True)
-            xg[:, k * piece : (k + 1) * piece] = (x * jnp.where(h == k % 2, near, far)).astype(jnp.bfloat16)
+                x = xbuf[m, 2 * peer(d) + hh].astype(jnp.float32)
+                total += jnp.sum(x * x, axis=1, keepdims=True)
+                xg[d - 1, :, hh * piece : (hh + 1) * piece] = gained(x, hh, part(peer(d)))
         scale[...] = jnp.broadcast_to(lax.rsqrt(total / full + epsilon), scale.shape)
 
         def chunk(c, _):
             @pl.when(m == 0)
             def _():
-                weight(c).wait()
-
-            @pl.when(m + 1 < units)
-            def _():
-                forward_chunk(m + 1, c)
-
-                @pl.when(c == chunks - 1)
-                def _():
-                    low_part(m + 1)
-
-            main = jnp.dot(xg[...], w[:, cols(c)], preferred_element_type=jnp.float32)
+                for d in range(1, tensors):
+                    far_weight(d, c).wait()
+
+            main = acc[:, cols(c)]
+            for d in range(1, tensors):
+                main += jnp.dot(xg[d - 1], w[far_rows(d), cols(c)], preferred_element_type=jnp.float32)
 
             @pl.when(c == 0)
             def _():
@@ -262,7 +302,7 @@
     units, rows = segment_ids.shape
     depth, piece = frozen.shape[1:]
     ranks = inbox_down.shape[3]
-    chunks = max(1, min(4, piece // 256))
+    chunks = max(1, min(2, piece // 256))
     step = piece // chunks
     bf16, f32 = jnp.bfloat16, jnp.float32
     anywhere = pl.BlockSpec(memory_space=pl.ANY)
@@ -281,7 +321,8 @@
         scratch_shapes=[
             pltpu.VMEM((depth, piece), bf16),
             pltpu.VMEM((units, 2 * tensors, rows, piece), bf16),
-            pltpu.VMEM((rows, depth), bf16),
+            pltpu.VMEM((max(1, tensors - 1), rows, 2 * piece), bf16),
+            pltpu.VMEM((rows, piece), f32),
             pltpu.VMEM((units, rows, piece), bf16),
             pltpu.VMEM(norm_gain.shape, bf16),
             pltpu.VMEM((tensors, piece, ranks), bf16),
@@ -291,7 +332,9 @@
             pltpu.VMEM((units, 2 * tensors, rows, ranks), f32),
             pltpu.VMEM((rows, ranks), bf16),
             pltpu.VMEM((rows, 128), f32),
-            dma((chunks,)),
+            pltpu.VMEM((rows, 128), f32),
+            dma((2, chunks)),
+            dma((tensors, chunks)),
             dma((units, 2, chunks)),
             dma((units, tensors, 2, chunks)),
             dma((units, tensors, 2, chunks)),

time: 138 us -> 132 us (0.957)
  Pallas kernels: 136 us -> 129 us
    pallas_call x1, Pallas kernels: 136 us -> 129 us  [local(): pl.pallas_call(body, out_shape=jax.ShapeDtypeStruct((1, units * rows, pie...]
where the time goes in v2:
time: 132 us; the launch traced here: 131 us
  Pallas kernels  129 us (98%)
  local copies, waits for them, and re-layouts  1.88 us (1%)
    pallas_call x1, Pallas kernels, local(): pl.pallas_call(body, out_shape=jax.ShapeDtypeStruct((1, units * rows, pie...  129 us

profile of v2, /device:TPU:28, one launch (start us, length us, event | category | flops | bytes accessed | tf_op | source)
XLA Modules:
  0.0 131.3 jit_solution(9186270179354619111)
XLA Ops:
  0.7 128.8 %shard_map.91 = bf16[1,128,2048]{2,1,0:T(8,128)(2,1)} custom-call(bf16[128,4096]{1,0:T(8,128)(2,1)} %hidden.1, s32[4,32]{1,0:T(4,128)} %ids.1, s32[4,8]{1,0:T(4,128)} %seg_job.1, s32[6]{0:T(128)} %job_ad.1, s32[1]{0:T(128)S(6)} %copy.11.owner, bf16[1,8192,2048]{2,1,0:T(8,128)(2,1)} %frozen.1, bf16[1,4096]{1,0:T(2,128)(2,1)} %gain.1, ...), custom_call_target="tpu_custom_call" | custom-call | tf_op jit(solution)/shard_map/pallas_call | solution.py:316
  129.4 1.9 %copy.12 = bf16[1,128,2048]{2,1,0:T(8,128)(2,1)} copy(bf16[1,128,2048]{2,1,0:T(8,128)(2,1)} %shard_map.91) | data formatting | bytes 1048576
